TPU v7x, 32 devices: a whole 2x2x4 slice. The times are simulated.
32 devices in a mesh: prow: 8 (over y, x, core), pcol: 4 (over z).
Axes of the slice: x: 2, y: 2, z: 4, core: 2. Of those that a mesh axis runs over, the one named last changes fastest.
Arguments:
- rhs: bfloat16 [128, 64, 256], P('prow'), may hold values from -6 to 6
- blocks: bfloat16 [128, 16, 256, 256], P('prow', 'pcol'), may hold values from -0.0625 to 0.0625
- inverses: bfloat16 [128, 256, 256], P('prow'), may hold values from -1 to 2.1, as said below
- columns: int32 [128, 16], P('prow', 'pcol'), may hold values from 0 to 127, as said below
- counts: int32 [128, 4], P('prow', 'pcol'), may hold values from 0 to 4, as said below
Outputs:
- solved: bfloat16 [128, 64, 256], P('prow')
Inputs may be any that keep to these rules, and one draw needn't show every extreme that they name: `columns`: slot c of array row o names a block row k (level order) of an earlier level than that of o, with (k // 8) % 4 == c // 4, or 0 where no such block row exists; only the first counts[o, c // 4] slots of a group are used. `counts`: 0 where the group has no earlier block row (level 0 in particular); otherwise 1 or more. `inverses`: each tile is the inverse of a lower triangular diagonal block, itself lower triangular.
All inputs are finite; a program needn't handle non-finite values.
Results may differ from a plain program's by a relative error of at most 0.0054.
Values may be sent and summed in bfloat16 or wider, within the bound.
No kernel may reach another device: no remote copies, remote signals or barrier semaphores. Data moves between devices by JAX's collectives and lax.ppermute only.
A program may use at most 64 MiB of HBM per device.

v0:
```python
import jax
import jax.numpy as jnp
from jax import lax
from jax.sharding import PartitionSpec as P

LEVELS = 8
LR = 2


def body(rhs, blocks, inverses, columns, counts):
    side_count = rhs.shape[1]
    block_size = rhs.shape[2]
    prow_count = lax.axis_size("prow")
    pcol_count = lax.axis_size("pcol")
    per_level = LR * prow_count
    slot_count = columns.shape[1]
    active_mask = (jnp.arange(slot_count, dtype=jnp.int32)[None, :] < counts).astype(jnp.bfloat16)
    store_rows = LEVELS * prow_count
    solved_store = jnp.zeros((store_rows, side_count, block_size), jnp.bfloat16)
    solution = jnp.zeros(rhs.shape, jnp.bfloat16)

    def advance(level_no, carry):
        solved_store, solution = carry
        first_row = level_no * LR
        column_ids = lax.dynamic_slice_in_dim(columns, first_row, LR, 0)
        active = lax.dynamic_slice_in_dim(active_mask, first_row, LR, 0)
        panels = lax.dynamic_slice_in_dim(blocks, first_row, LR, 0)
        right_side = lax.dynamic_slice_in_dim(rhs, first_row, LR, 0)
        inverse_tiles = lax.dynamic_slice_in_dim(inverses, first_row, LR, 0)
        store_ids = column_ids // per_level * prow_count + column_ids % prow_count
        gathered = jnp.take(solved_store, store_ids, axis=0) * active[:, :, None, None]
        update_sum = jnp.einsum(
            "scrj,scij->sri", gathered, panels, preferred_element_type=jnp.float32
        )
        which_half = (lax.axis_index("pcol") - level_no * LR) % pcol_count
        keep_half = (which_half < LR).astype(jnp.bfloat16)
        half_index = jnp.minimum(which_half, LR - 1)
        summed = lax.psum(update_sum, "pcol")
        residual = (right_side.astype(jnp.float32) - summed).astype(jnp.bfloat16)
        solved_now = jnp.einsum(
            "srb,sab->sra", residual, inverse_tiles, preferred_element_type=jnp.float32
        ).astype(jnp.bfloat16)
        payload = lax.dynamic_index_in_dim(solved_now, half_index, 0, keepdims=True) * keep_half
        level_block = lax.all_gather(payload[None], "prow", axis=0, tiled=True)
        column_block = level_block.reshape((prow_count, side_count, block_size))
        solved_store = lax.dynamic_update_slice_in_dim(
            solved_store, column_block, level_no * prow_count, 0
        )
        solution = lax.dynamic_update_slice_in_dim(solution, solved_now, first_row, 0)
        return (solved_store, solution)

    solved_store, solution = lax.fori_loop(0, LEVELS, advance, (solved_store, solution))
    return solution


def solution(mesh):
    placed = (
        P("prow", None, None),
        P("prow", "pcol", None, None),
        P("prow", None, None),
        P("prow", "pcol"),
        P("prow", "pcol"),
    )
    return jax.shard_map(
        body, mesh=mesh, in_specs=placed, out_specs=P("prow", None, None), check_vma=False
    )
```

profile of v0, /device:TPU:0, one launch (start us, length us, event | category | flops | bytes accessed | tf_op | source)
XLA Modules:
  0.0 398.1 jit_solution(2024207592908420231)
XLA Ops:
  8.3 382.1 %while.18 = (s32[]{:T(128)}, bf16[64,64,256]{2,1,0:T(8,128)(2,1)S(1)}, bf16[16,64,256]{2,1,0:T(8,128)(2,1)S(1)}, bf16[16,64,256]{2,1,0:T(8,128)(2,1)}, s32[16,4]...) while((s32[]{:T(128)}, ...), condition=%wide.region_2.3_spmd, body=%wide.region_0.2_spmd.sunk | while | flops 84329728 | bytes 4233478 | solution.py:52
  9.1 2.3 convolution_bitcast_fusion.2
  11.5 37.5 %all-reduce.2.cloned.1.call-done = f32[2,64,256]{2,1,0:T(8,128)} async-done(((f32[2,64,256]{2,1,0:T(8,128)}), f32[2,64,256]{2,1,0:T(8,128)}) %all-reduce.2.cloned.1.call-update) | async-done | bytes 131088 | tf_op jit(solution)/shard_map/while/body/eval_jaxpr/psum | solution.py:38
  49.0 1.3 constant_dynamic-update-slice_fusion.4
  50.2 9.2 %all-gather.2 = bf16[8,64,256]{2,1,0:T(8,128)(2,1)S(1)} all-gather(bf16[1,64,256]{2,1,0:T(8,128)(2,1)S(1)} %dynamic-slice_multiply_fusion.2), channel_id=2, replica_groups=mesh['prow'=8,'pcol'=4] {'prow'}, dimensions={0}, use_global_device_ids=true | all-gather | bytes 294912 | tf_op jit(solution)/shard_map/while/body/eval_jaxpr/all_gather | solution.py:44
  60.3 2.3 convolution_bitcast_fusion.2
  62.7 33.6 %all-reduce.2.cloned.1.call-done = f32[2,64,256]{2,1,0:T(8,128)} async-done(((f32[2,64,256]{2,1,0:T(8,128)}), f32[2,64,256]{2,1,0:T(8,128)}) %all-reduce.2.cloned.1.call-update) | async-done | bytes 131088 | tf_op jit(solution)/shard_map/while/body/eval_jaxpr/psum | solution.py:38
  96.2 1.3 constant_dynamic-update-slice_fusion.4
  97.5 9.2 %all-gather.2 = bf16[8,64,256]{2,1,0:T(8,128)(2,1)S(1)} all-gather(bf16[1,64,256]{2,1,0:T(8,128)(2,1)S(1)} %dynamic-slice_multiply_fusion.2), channel_id=2, replica_groups=mesh['prow'=8,'pcol'=4] {'prow'}, dimensions={0}, use_global_device_ids=true | all-gather | bytes 294912 | tf_op jit(solution)/shard_map/while/body/eval_jaxpr/all_gather | solution.py:44
  107.6 2.3 convolution_bitcast_fusion.2
  110.0 33.5 %all-reduce.2.cloned.1.call-done = f32[2,64,256]{2,1,0:T(8,128)} async-done(((f32[2,64,256]{2,1,0:T(8,128)}), f32[2,64,256]{2,1,0:T(8,128)}) %all-reduce.2.cloned.1.call-update) | async-done | bytes 131088 | tf_op jit(solution)/shard_map/while/body/eval_jaxpr/psum | solution.py:38
  143.5 1.3 constant_dynamic-update-slice_fusion.4
  144.8 9.2 %all-gather.2 = bf16[8,64,256]{2,1,0:T(8,128)(2,1)S(1)} all-gather(bf16[1,64,256]{2,1,0:T(8,128)(2,1)S(1)} %dynamic-slice_multiply_fusion.2), channel_id=2, replica_groups=mesh['prow'=8,'pcol'=4] {'prow'}, dimensions={0}, use_global_device_ids=true | all-gather | bytes 294912 | tf_op jit(solution)/shard_map/while/body/eval_jaxpr/all_gather | solution.py:44
  154.8 2.3 convolution_bitcast_fusion.2
  157.2 33.5 %all-reduce.2.cloned.1.call-done = f32[2,64,256]{2,1,0:T(8,128)} async-done(((f32[2,64,256]{2,1,0:T(8,128)}), f32[2,64,256]{2,1,0:T(8,128)}) %all-reduce.2.cloned.1.call-update) | async-done | bytes 131088 | tf_op jit(solution)/shard_map/while/body/eval_jaxpr/psum | solution.py:38
  190.8 1.3 constant_dynamic-update-slice_fusion.4
  192.1 9.2 %all-gather.2 = bf16[8,64,256]{2,1,0:T(8,128)(2,1)S(1)} all-gather(bf16[1,64,256]{2,1,0:T(8,128)(2,1)S(1)} %dynamic-slice_multiply_fusion.2), channel_id=2, replica_groups=mesh['prow'=8,'pcol'=4] {'prow'}, dimensions={0}, use_global_device_ids=true | all-gather | bytes 294912 | tf_op jit(solution)/shard_map/while/body/eval_jaxpr/all_gather | solution.py:44
  202.1 2.3 convolution_bitcast_fusion.2
  204.5 33.5 %all-reduce.2.cloned.1.call-done = f32[2,64,256]{2,1,0:T(8,128)} async-done(((f32[2,64,256]{2,1,0:T(8,128)}), f32[2,64,256]{2,1,0:T(8,128)}) %all-reduce.2.cloned.1.call-update) | async-done | bytes 131088 | tf_op jit(solution)/shard_map/while/body/eval_jaxpr/psum | solution.py:38
  238.1 1.3 constant_dynamic-update-slice_fusion.4
  239.3 9.2 %all-gather.2 = bf16[8,64,256]{2,1,0:T(8,128)(2,1)S(1)} all-gather(bf16[1,64,256]{2,1,0:T(8,128)(2,1)S(1)} %dynamic-slice_multiply_fusion.2), channel_id=2, replica_groups=mesh['prow'=8,'pcol'=4] {'prow'}, dimensions={0}, use_global_device_ids=true | all-gather | bytes 294912 | tf_op jit(solution)/shard_map/while/body/eval_jaxpr/all_gather | solution.py:44
  249.4 2.3 convolution_bitcast_fusion.2
  251.8 33.5 %all-reduce.2.cloned.1.call-done = f32[2,64,256]{2,1,0:T(8,128)} async-done(((f32[2,64,256]{2,1,0:T(8,128)}), f32[2,64,256]{2,1,0:T(8,128)}) %all-reduce.2.cloned.1.call-update) | async-done | bytes 131088 | tf_op jit(solution)/shard_map/while/body/eval_jaxpr/psum | solution.py:38
  285.3 1.3 constant_dynamic-update-slice_fusion.4
  286.6 9.2 %all-gather.2 = bf16[8,64,256]{2,1,0:T(8,128)(2,1)S(1)} all-gather(bf16[1,64,256]{2,1,0:T(8,128)(2,1)S(1)} %dynamic-slice_multiply_fusion.2), channel_id=2, replica_groups=mesh['prow'=8,'pcol'=4] {'prow'}, dimensions={0}, use_global_device_ids=true | all-gather | bytes 294912 | tf_op jit(solution)/shard_map/while/body/eval_jaxpr/all_gather | solution.py:44
  296.7 2.3 convolution_bitcast_fusion.2
  299.1 33.5 %all-reduce.2.cloned.1.call-done = f32[2,64,256]{2,1,0:T(8,128)} async-done(((f32[2,64,256]{2,1,0:T(8,128)}), f32[2,64,256]{2,1,0:T(8,128)}) %all-reduce.2.cloned.1.call-update) | async-done | bytes 131088 | tf_op jit(solution)/shard_map/while/body/eval_jaxpr/psum | solution.py:38
  333.9 9.2 %all-gather.2 = bf16[8,64,256]{2,1,0:T(8,128)(2,1)S(1)} all-gather(bf16[1,64,256]{2,1,0:T(8,128)(2,1)S(1)} %dynamic-slice_multiply_fusion.2), channel_id=2, replica_groups=mesh['prow'=8,'pcol'=4] {'prow'}, dimensions={0}, use_global_device_ids=true | all-gather | bytes 294912 | tf_op jit(solution)/shard_map/while/body/eval_jaxpr/all_gather | solution.py:44
  343.9 2.3 convolution_bitcast_fusion.2
  346.4 33.5 %all-reduce.2.cloned.1.call-done = f32[2,64,256]{2,1,0:T(8,128)} async-done(((f32[2,64,256]{2,1,0:T(8,128)}), f32[2,64,256]{2,1,0:T(8,128)}) %all-reduce.2.cloned.1.call-update) | async-done | bytes 131088 | tf_op jit(solution)/shard_map/while/body/eval_jaxpr/psum | solution.py:38
  379.9 1.3 constant_dynamic-update-slice_fusion.4
  381.2 9.2 %all-gather.2 = bf16[8,64,256]{2,1,0:T(8,128)(2,1)S(1)} all-gather(bf16[1,64,256]{2,1,0:T(8,128)(2,1)S(1)} %dynamic-slice_multiply_fusion.2), channel_id=2, replica_groups=mesh['prow'=8,'pcol'=4] {'prow'}, dimensions={0}, use_global_device_ids=true | all-gather | bytes 294912 | tf_op jit(solution)/shard_map/while/body/eval_jaxpr/all_gather | solution.py:44
  (79 shorter events, 10.1 us)
Async XLA Ops:
  8.3 40.6 %all-reduce.2.cloned.1.call-start = ((), (), s32[]{:S(2)}) async-start(), calls=%async_computation | async-start | bytes 262144 | tf_op jit(solution)/shard_map/while/body/eval_jaxpr/psum | solution.py:38
  59.5 36.7 %all-reduce.2.cloned.1.call-start = ((), (), s32[]{:S(2)}) async-start(), calls=%async_computation | async-start | bytes 262144 | tf_op jit(solution)/shard_map/while/body/eval_jaxpr/psum | solution.py:38
  106.8 36.7 %all-reduce.2.cloned.1.call-start = ((), (), s32[]{:S(2)}) async-start(), calls=%async_computation | async-start | bytes 262144 | tf_op jit(solution)/shard_map/while/body/eval_jaxpr/psum | solution.py:38
  154.1 36.7 %all-reduce.2.cloned.1.call-start = ((), (), s32[]{:S(2)}) async-start(), calls=%async_computation | async-start | bytes 262144 | tf_op jit(solution)/shard_map/while/body/eval_jaxpr/psum | solution.py:38
  201.4 36.7 %all-reduce.2.cloned.1.call-start = ((), (), s32[]{:S(2)}) async-start(), calls=%async_computation | async-start | bytes 262144 | tf_op jit(solution)/shard_map/while/body/eval_jaxpr/psum | solution.py:38
  248.6 36.7 %all-reduce.2.cloned.1.call-start = ((), (), s32[]{:S(2)}) async-start(), calls=%async_computation | async-start | bytes 262144 | tf_op jit(solution)/shard_map/while/body/eval_jaxpr/psum | solution.py:38
  295.9 36.7 %all-reduce.2.cloned.1.call-start = ((), (), s32[]{:S(2)}) async-start(), calls=%async_computation | async-start | bytes 262144 | tf_op jit(solution)/shard_map/while/body/eval_jaxpr/psum | solution.py:38
  343.2 36.7 %all-reduce.2.cloned.1.call-start = ((), (), s32[]{:S(2)}) async-start(), calls=%async_computation | async-start | bytes 262144 | tf_op jit(solution)/shard_map/while/body/eval_jaxpr/psum | solution.py:38
  390.4 0.8 copy-start
Sparse Core Ops, SparseCore 0:
  11.6 37.3 all-reduce.1
  62.8 33.4 all-reduce.1
  110.1 33.4 all-reduce.1
  157.3 33.4 all-reduce.1
  204.6 33.4 all-reduce.1
  251.9 33.4 all-reduce.1
  299.2 33.4 all-reduce.1
  346.4 33.4 all-reduce.1
where the time goes:
time: 399 us; the launch traced here: 398 us
  waiting for transfers between devices  272 us (68%)
  blocking collectives  74 us (19%)
  matrix products  28.7 us (7%)
  between operations  13.4 us (3%)
  local copies, waits for them, and re-layouts  7.25 us (2%)
    psum x8, waiting for transfers between devices, advance(): summed = lax.psum(update_sum, 'pcol')  272 us
    all_gather x8, blocking collectives, advance(): level_block = lax.all_gather(payload[None], 'prow', axis=0, tiled=True)  74 us
    dot_general x8, matrix products, advance(): jnp.einsum('scrj,scij->sri', gathered, panels, preferred_element_type=jnp...  18.7 us
    dot_general x8, matrix products, advance(): jnp.einsum('srb,sab->sra', residual, inverse_tiles, preferred_element_typ...  10 us
  transfers between devices with their start and end apart: 8, of which 8 were waited for; matrix products, arithmetic and copies ran while one was open for 0% of the time, Pallas kernels for 0%

commit v1 on v0

--- a/solution.py
+++ b/solution.py
@@ -35,7 +35,9 @@
         which_half = (lax.axis_index("pcol") - level_no * LR) % pcol_count
         keep_half = (which_half < LR).astype(jnp.bfloat16)
         half_index = jnp.minimum(which_half, LR - 1)
-        summed = lax.psum(update_sum, "pcol")
+        summed = update_sum
+        for hop in (1, 2):
+            summed = summed + lax.ppermute(summed, "pcol", [(dev, dev ^ hop) for dev in range(4)])
         residual = (right_side.astype(jnp.float32) - summed).astype(jnp.bfloat16)
         solved_now = jnp.einsum(
             "srb,sab->sra", residual, inverse_tiles, preferred_element_type=jnp.float32

time: 399 us -> 220 us (0.55)
  waiting for transfers between devices: 272 us -> 88.7 us
  starting transfers between devices: 0.33 us -> 27.7 us
  between operations: 13.4 us -> 0.03 us
  matrix products: 28.7 us -> 22.9 us
    psum x8 -> x0, waiting for transfers between devices: 272 us -> none  [advance(): summed = lax.psum(update_sum, 'pcol')]
    ppermute x0 -> x16, waiting for transfers between devices: none -> 88.7 us  [advance(): lax.ppermute(summed, 'pcol', [(dev, dev ^ hop) for dev in range(4)])]
    ppermute x0 -> x16, starting transfers between devices: none -> 27.7 us  [advance(): lax.ppermute(summed, 'pcol', [(dev, dev ^ hop) for dev in range(4)])]
    dot_general x8, matrix products: 18.7 us -> 13.4 us  [advance(): jnp.einsum('scrj,scij->sri', gathered, panels, preferred_element_type=jnp...]
  transfers between devices with their start and end apart: 8 -> 16, of which waited for: 8 -> 16; matrix products, arithmetic and copies ran while one was open for 0% -> 0% of each run, Pallas kernels for 0% -> 0%
where the time goes in v1:
time: 220 us
  waiting for transfers between devices  88.7 us (40%)
  blocking collectives  71.3 us (32%)
  starting transfers between devices  27.7 us (13%)
  matrix products  22.9 us (10%)
  local copies, waits for them, and re-layouts  7.25 us (3%)
    ppermute x16, waiting for transfers between devices, advance(): lax.ppermute(summed, 'pcol', [(dev, dev ^ hop) for dev in range(4)])  88.7 us
    all_gather x8, blocking collectives, advance(): level_block = lax.all_gather(payload[None], 'prow', axis=0, tiled=True)  71.3 us
    ppermute x16, starting transfers between devices, advance(): lax.ppermute(summed, 'pcol', [(dev, dev ^ hop) for dev in range(4)])  27.7 us
    dot_general x8, matrix products, advance(): jnp.einsum('scrj,scij->sri', gathered, panels, preferred_element_type=jnp...  13.4 us
    dot_general x8, matrix products, advance(): jnp.einsum('srb,sab->sra', residual, inverse_tiles, preferred_element_typ...  9.53 us
    gather x8, local copies, waits for them, and re-layouts, advance(): jnp.take(solved_store, store_ids, axis=0) * active[:, :, None, None]  4.5 us
  transfers between devices with their start and end apart: 16, of which 16 were waited for; matrix products, arithmetic and copies ran while one was open for 0% of the time, Pallas kernels for 0%

profile of v1, /device:TPU:0, one launch (start us, length us, event | category | flops | bytes accessed | tf_op | source)
XLA Modules:
  0.0 219.7 jit_solution(13621038159217790067)
XLA Ops:
  1.8 217.1 %while.18 = (s32[]{:T(128)}, bf16[64,64,256]{2,1,0:T(8,128)(2,1)S(1)}, bf16[16,64,256]{2,1,0:T(8,128)(2,1)S(1)}, bf16[16,64,256]{2,1,0:T(8,128)(2,1)}, s32[16,4]...) while((s32[]{:T(128)}, ...), condition=%wide.region_1.2_spmd, body=%wide.region_0.1_spmd.sunk | while | flops 84362496 | bytes 5019950 | solution.py:54
  4.2 3.1 %collective-permute-start = (f32[2,64,256]{2,1,0:T(8,128)S(1)}, f32[2,64,256]{2,1,0:T(8,128)S(1)}, u32[]{:S(2)}, u32[]{:S(2)}) collective-permute-start(f32[2,64,256]{2,1,0:T(8,128)S(1)} %convolution_bitcast_fusion.2), channel_id=1, source_target_pairs={{0,1},{1,0},{2,3},{3,2},{4,5},{5,4},{6,7},{7,6},{8,9},{9,8},{10,11... | collective-permute-start | bytes 393224 | tf_op jit(solution)/shard_map/while/body/eval_jaxpr/ppermute | solution.py:40
  7.3 3.5 %collective-permute-done = f32[2,64,256]{2,1,0:T(8,128)S(1)} collective-permute-done((f32[2,64,256]{2,1,0:T(8,128)S(1)}, f32[2,64,256]{2,1,0:T(8,128)S(1)}, u32[]{:S(2)}, u32[]{:S(2)}) %collective-permute-start) | collective-permute-done | bytes 131104 | tf_op jit(solution)/shard_map/while/body/eval_jaxpr/ppermute | solution.py:40
  10.8 2.8 %collective-permute-start.1 = (f32[2,64,256]{2,1,0:T(8,128)S(1)}, f32[2,64,256]{2,1,0:T(8,128)S(1)}, u32[]{:S(2)}, u32[]{:S(2)}) collective-permute-start(f32[2,64,256]{2,1,0:T(8,128)S(1)} %add.164), channel_id=1, source_target_pairs={{0,2},{1,3},{2,0},{3,1},{4,6},{5,7},{6,4},{7,5},{8,10},{9,11},{10,... | collective-permute-start | bytes 393224 | tf_op jit(solution)/shard_map/while/body/eval_jaxpr/ppermute | solution.py:40
  13.7 5.6 %collective-permute-done.1 = f32[2,64,256]{2,1,0:T(8,128)S(1)} collective-permute-done((f32[2,64,256]{2,1,0:T(8,128)S(1)}, f32[2,64,256]{2,1,0:T(8,128)S(1)}, u32[]{:S(2)}, u32[]{:S(2)}) %collective-permute-start.1) | collective-permute-done | bytes 131104 | tf_op jit(solution)/shard_map/while/body/eval_jaxpr/ppermute | solution.py:40
  20.5 9.2 %all-gather.2 = bf16[8,64,256]{2,1,0:T(8,128)(2,1)S(1)} all-gather(bf16[1,64,256]{2,1,0:T(8,128)(2,1)S(1)} %dynamic-slice_multiply_fusion.2), channel_id=2, replica_groups=mesh['prow'=8,'pcol'=4] {'prow'}, dimensions={0}, use_global_device_ids=true | all-gather | bytes 294912 | tf_op jit(solution)/shard_map/while/body/eval_jaxpr/all_gather | solution.py:46
  32.8 5.1 %collective-permute-done = f32[2,64,256]{2,1,0:T(8,128)S(1)} collective-permute-done((f32[2,64,256]{2,1,0:T(8,128)S(1)}, f32[2,64,256]{2,1,0:T(8,128)S(1)}, u32[]{:S(2)}, u32[]{:S(2)}) %collective-permute-start) | collective-permute-done | bytes 131104 | tf_op jit(solution)/shard_map/while/body/eval_jaxpr/ppermute | solution.py:40
  37.9 2.4 %collective-permute-start.1 = (f32[2,64,256]{2,1,0:T(8,128)S(1)}, f32[2,64,256]{2,1,0:T(8,128)S(1)}, u32[]{:S(2)}, u32[]{:S(2)}) collective-permute-start(f32[2,64,256]{2,1,0:T(8,128)S(1)} %add.164), channel_id=1, source_target_pairs={{0,2},{1,3},{2,0},{3,1},{4,6},{5,7},{6,4},{7,5},{8,10},{9,11},{10,... | collective-permute-start | bytes 393224 | tf_op jit(solution)/shard_map/while/body/eval_jaxpr/ppermute | solution.py:40
  40.3 6.3 %collective-permute-done.1 = f32[2,64,256]{2,1,0:T(8,128)S(1)} collective-permute-done((f32[2,64,256]{2,1,0:T(8,128)S(1)}, f32[2,64,256]{2,1,0:T(8,128)S(1)}, u32[]{:S(2)}, u32[]{:S(2)}) %collective-permute-start.1) | collective-permute-done | bytes 131104 | tf_op jit(solution)/shard_map/while/body/eval_jaxpr/ppermute | solution.py:40
  47.8 9.3 %all-gather.2 = bf16[8,64,256]{2,1,0:T(8,128)(2,1)S(1)} all-gather(bf16[1,64,256]{2,1,0:T(8,128)(2,1)S(1)} %dynamic-slice_multiply_fusion.2), channel_id=2, replica_groups=mesh['prow'=8,'pcol'=4] {'prow'}, dimensions={0}, use_global_device_ids=true | all-gather | bytes 294912 | tf_op jit(solution)/shard_map/while/body/eval_jaxpr/all_gather | solution.py:46
  60.3 5.1 %collective-permute-done = f32[2,64,256]{2,1,0:T(8,128)S(1)} collective-permute-done((f32[2,64,256]{2,1,0:T(8,128)S(1)}, f32[2,64,256]{2,1,0:T(8,128)S(1)}, u32[]{:S(2)}, u32[]{:S(2)}) %collective-permute-start) | collective-permute-done | bytes 131104 | tf_op jit(solution)/shard_map/while/body/eval_jaxpr/ppermute | solution.py:40
  65.4 2.4 %collective-permute-start.1 = (f32[2,64,256]{2,1,0:T(8,128)S(1)}, f32[2,64,256]{2,1,0:T(8,128)S(1)}, u32[]{:S(2)}, u32[]{:S(2)}) collective-permute-start(f32[2,64,256]{2,1,0:T(8,128)S(1)} %add.164), channel_id=1, source_target_pairs={{0,2},{1,3},{2,0},{3,1},{4,6},{5,7},{6,4},{7,5},{8,10},{9,11},{10,... | collective-permute-start | bytes 393224 | tf_op jit(solution)/shard_map/while/body/eval_jaxpr/ppermute | solution.py:40
  67.8 6.3 %collective-permute-done.1 = f32[2,64,256]{2,1,0:T(8,128)S(1)} collective-permute-done((f32[2,64,256]{2,1,0:T(8,128)S(1)}, f32[2,64,256]{2,1,0:T(8,128)S(1)}, u32[]{:S(2)}, u32[]{:S(2)}) %collective-permute-start.1) | collective-permute-done | bytes 131104 | tf_op jit(solution)/shard_map/while/body/eval_jaxpr/ppermute | solution.py:40
  75.3 8.3 %all-gather.2 = bf16[8,64,256]{2,1,0:T(8,128)(2,1)S(1)} all-gather(bf16[1,64,256]{2,1,0:T(8,128)(2,1)S(1)} %dynamic-slice_multiply_fusion.2), channel_id=2, replica_groups=mesh['prow'=8,'pcol'=4] {'prow'}, dimensions={0}, use_global_device_ids=true | all-gather | bytes 294912 | tf_op jit(solution)/shard_map/while/body/eval_jaxpr/all_gather | solution.py:46
  86.8 5.1 %collective-permute-done = f32[2,64,256]{2,1,0:T(8,128)S(1)} collective-permute-done((f32[2,64,256]{2,1,0:T(8,128)S(1)}, f32[2,64,256]{2,1,0:T(8,128)S(1)}, u32[]{:S(2)}, u32[]{:S(2)}) %collective-permute-start) | collective-permute-done | bytes 131104 | tf_op jit(solution)/shard_map/while/body/eval_jaxpr/ppermute | solution.py:40
  91.9 2.4 %collective-permute-start.1 = (f32[2,64,256]{2,1,0:T(8,128)S(1)}, f32[2,64,256]{2,1,0:T(8,128)S(1)}, u32[]{:S(2)}, u32[]{:S(2)}) collective-permute-start(f32[2,64,256]{2,1,0:T(8,128)S(1)} %add.164), channel_id=1, source_target_pairs={{0,2},{1,3},{2,0},{3,1},{4,6},{5,7},{6,4},{7,5},{8,10},{9,11},{10,... | collective-permute-start | bytes 393224 | tf_op jit(solution)/shard_map/while/body/eval_jaxpr/ppermute | solution.py:40
  94.2 6.3 %collective-permute-done.1 = f32[2,64,256]{2,1,0:T(8,128)S(1)} collective-permute-done((f32[2,64,256]{2,1,0:T(8,128)S(1)}, f32[2,64,256]{2,1,0:T(8,128)S(1)}, u32[]{:S(2)}, u32[]{:S(2)}) %collective-permute-start.1) | collective-permute-done | bytes 131104 | tf_op jit(solution)/shard_map/while/body/eval_jaxpr/ppermute | solution.py:40
  101.7 9.3 %all-gather.2 = bf16[8,64,256]{2,1,0:T(8,128)(2,1)S(1)} all-gather(bf16[1,64,256]{2,1,0:T(8,128)(2,1)S(1)} %dynamic-slice_multiply_fusion.2), channel_id=2, replica_groups=mesh['prow'=8,'pcol'=4] {'prow'}, dimensions={0}, use_global_device_ids=true | all-gather | bytes 294912 | tf_op jit(solution)/shard_map/while/body/eval_jaxpr/all_gather | solution.py:46
  114.2 5.1 %collective-permute-done = f32[2,64,256]{2,1,0:T(8,128)S(1)} collective-permute-done((f32[2,64,256]{2,1,0:T(8,128)S(1)}, f32[2,64,256]{2,1,0:T(8,128)S(1)}, u32[]{:S(2)}, u32[]{:S(2)}) %collective-permute-start) | collective-permute-done | bytes 131104 | tf_op jit(solution)/shard_map/while/body/eval_jaxpr/ppermute | solution.py:40
  121.7 6.3 %collective-permute-done.1 = f32[2,64,256]{2,1,0:T(8,128)S(1)} collective-permute-done((f32[2,64,256]{2,1,0:T(8,128)S(1)}, f32[2,64,256]{2,1,0:T(8,128)S(1)}, u32[]{:S(2)}, u32[]{:S(2)}) %collective-permute-start.1) | collective-permute-done | bytes 131104 | tf_op jit(solution)/shard_map/while/body/eval_jaxpr/ppermute | solution.py:40
  129.2 8.3 %all-gather.2 = bf16[8,64,256]{2,1,0:T(8,128)(2,1)S(1)} all-gather(bf16[1,64,256]{2,1,0:T(8,128)(2,1)S(1)} %dynamic-slice_multiply_fusion.2), channel_id=2, replica_groups=mesh['prow'=8,'pcol'=4] {'prow'}, dimensions={0}, use_global_device_ids=true | all-gather | bytes 294912 | tf_op jit(solution)/shard_map/while/body/eval_jaxpr/all_gather | solution.py:46
  140.7 5.1 %collective-permute-done = f32[2,64,256]{2,1,0:T(8,128)S(1)} collective-permute-done((f32[2,64,256]{2,1,0:T(8,128)S(1)}, f32[2,64,256]{2,1,0:T(8,128)S(1)}, u32[]{:S(2)}, u32[]{:S(2)}) %collective-permute-start) | collective-permute-done | bytes 131104 | tf_op jit(solution)/shard_map/while/body/eval_jaxpr/ppermute | solution.py:40
  145.8 2.4 %collective-permute-start.1 = (f32[2,64,256]{2,1,0:T(8,128)S(1)}, f32[2,64,256]{2,1,0:T(8,128)S(1)}, u32[]{:S(2)}, u32[]{:S(2)}) collective-permute-start(f32[2,64,256]{2,1,0:T(8,128)S(1)} %add.164), channel_id=1, source_target_pairs={{0,2},{1,3},{2,0},{3,1},{4,6},{5,7},{6,4},{7,5},{8,10},{9,11},{10,... | collective-permute-start | bytes 393224 | tf_op jit(solution)/shard_map/while/body/eval_jaxpr/ppermute | solution.py:40
  148.2 6.3 %collective-permute-done.1 = f32[2,64,256]{2,1,0:T(8,128)S(1)} collective-permute-done((f32[2,64,256]{2,1,0:T(8,128)S(1)}, f32[2,64,256]{2,1,0:T(8,128)S(1)}, u32[]{:S(2)}, u32[]{:S(2)}) %collective-permute-start.1) | collective-permute-done | bytes 131104 | tf_op jit(solution)/shard_map/while/body/eval_jaxpr/ppermute | solution.py:40
  155.7 9.3 %all-gather.2 = bf16[8,64,256]{2,1,0:T(8,128)(2,1)S(1)} all-gather(bf16[1,64,256]{2,1,0:T(8,128)(2,1)S(1)} %dynamic-slice_multiply_fusion.2), channel_id=2, replica_groups=mesh['prow'=8,'pcol'=4] {'prow'}, dimensions={0}, use_global_device_ids=true | all-gather | bytes 294912 | tf_op jit(solution)/shard_map/while/body/eval_jaxpr/all_gather | solution.py:46
  168.1 5.1 %collective-permute-done = f32[2,64,256]{2,1,0:T(8,128)S(1)} collective-permute-done((f32[2,64,256]{2,1,0:T(8,128)S(1)}, f32[2,64,256]{2,1,0:T(8,128)S(1)}, u32[]{:S(2)}, u32[]{:S(2)}) %collective-permute-start) | collective-permute-done | bytes 131104 | tf_op jit(solution)/shard_map/while/body/eval_jaxpr/ppermute | solution.py:40
  175.6 6.3 %collective-permute-done.1 = f32[2,64,256]{2,1,0:T(8,128)S(1)} collective-permute-done((f32[2,64,256]{2,1,0:T(8,128)S(1)}, f32[2,64,256]{2,1,0:T(8,128)S(1)}, u32[]{:S(2)}, u32[]{:S(2)}) %collective-permute-start.1) | collective-permute-done | bytes 131104 | tf_op jit(solution)/shard_map/while/body/eval_jaxpr/ppermute | solution.py:40
  183.1 8.3 %all-gather.2 = bf16[8,64,256]{2,1,0:T(8,128)(2,1)S(1)} all-gather(bf16[1,64,256]{2,1,0:T(8,128)(2,1)S(1)} %dynamic-slice_multiply_fusion.2), channel_id=2, replica_groups=mesh['prow'=8,'pcol'=4] {'prow'}, dimensions={0}, use_global_device_ids=true | all-gather | bytes 294912 | tf_op jit(solution)/shard_map/while/body/eval_jaxpr/all_gather | solution.py:46
  194.6 5.1 %collective-permute-done = f32[2,64,256]{2,1,0:T(8,128)S(1)} collective-permute-done((f32[2,64,256]{2,1,0:T(8,128)S(1)}, f32[2,64,256]{2,1,0:T(8,128)S(1)}, u32[]{:S(2)}, u32[]{:S(2)}) %collective-permute-start) | collective-permute-done | bytes 131104 | tf_op jit(solution)/shard_map/while/body/eval_jaxpr/ppermute | solution.py:40
  199.7 2.4 %collective-permute-start.1 = (f32[2,64,256]{2,1,0:T(8,128)S(1)}, f32[2,64,256]{2,1,0:T(8,128)S(1)}, u32[]{:S(2)}, u32[]{:S(2)}) collective-permute-start(f32[2,64,256]{2,1,0:T(8,128)S(1)} %add.164), channel_id=1, source_target_pairs={{0,2},{1,3},{2,0},{3,1},{4,6},{5,7},{6,4},{7,5},{8,10},{9,11},{10,... | collective-permute-start | bytes 393224 | tf_op jit(solution)/shard_map/while/body/eval_jaxpr/ppermute | solution.py:40
  202.1 6.3 %collective-permute-done.1 = f32[2,64,256]{2,1,0:T(8,128)S(1)} collective-permute-done((f32[2,64,256]{2,1,0:T(8,128)S(1)}, f32[2,64,256]{2,1,0:T(8,128)S(1)}, u32[]{:S(2)}, u32[]{:S(2)}) %collective-permute-start.1) | collective-permute-done | bytes 131104 | tf_op jit(solution)/shard_map/while/body/eval_jaxpr/ppermute | solution.py:40
  209.6 9.3 %all-gather.2 = bf16[8,64,256]{2,1,0:T(8,128)(2,1)S(1)} all-gather(bf16[1,64,256]{2,1,0:T(8,128)(2,1)S(1)} %dynamic-slice_multiply_fusion.2), channel_id=2, replica_groups=mesh['prow'=8,'pcol'=4] {'prow'}, dimensions={0}, use_global_device_ids=true | all-gather | bytes 294912 | tf_op jit(solution)/shard_map/while/body/eval_jaxpr/all_gather | solution.py:46
  (95 shorter events, 41.3 us)
Async XLA Ops:
  4.2 6.6 %collective-permute-start = (f32[2,64,256]{2,1,0:T(8,128)S(1)}, f32[2,64,256]{2,1,0:T(8,128)S(1)}, u32[]{:S(2)}, u32[]{:S(2)}) collective-permute-start(f32[2,64,256]{2,1,0:T(8,128)S(1)} %convolution_bitcast_fusion.2), channel_id=1, source_target_pairs={{0,1},{1,0},{2,3},{3,2},{4,5},{5,4},{6,7},{7,6},{8,9},{9,8},{10,11... | collective-permute-start | bytes 393224 | tf_op jit(solution)/shard_map/while/body/eval_jaxpr/ppermute | solution.py:40
  10.8 8.4 %collective-permute-start.1 = (f32[2,64,256]{2,1,0:T(8,128)S(1)}, f32[2,64,256]{2,1,0:T(8,128)S(1)}, u32[]{:S(2)}, u32[]{:S(2)}) collective-permute-start(f32[2,64,256]{2,1,0:T(8,128)S(1)} %add.164), channel_id=1, source_target_pairs={{0,2},{1,3},{2,0},{3,1},{4,6},{5,7},{6,4},{7,5},{8,10},{9,11},{10,... | collective-permute-start | bytes 393224 | tf_op jit(solution)/shard_map/while/body/eval_jaxpr/ppermute | solution.py:40
  32.1 5.8 %collective-permute-start = (f32[2,64,256]{2,1,0:T(8,128)S(1)}, f32[2,64,256]{2,1,0:T(8,128)S(1)}, u32[]{:S(2)}, u32[]{:S(2)}) collective-permute-start(f32[2,64,256]{2,1,0:T(8,128)S(1)} %convolution_bitcast_fusion.2), channel_id=1, source_target_pairs={{0,1},{1,0},{2,3},{3,2},{4,5},{5,4},{6,7},{7,6},{8,9},{9,8},{10,11... | collective-permute-start | bytes 393224 | tf_op jit(solution)/shard_map/while/body/eval_jaxpr/ppermute | solution.py:40
  37.9 8.7 %collective-permute-start.1 = (f32[2,64,256]{2,1,0:T(8,128)S(1)}, f32[2,64,256]{2,1,0:T(8,128)S(1)}, u32[]{:S(2)}, u32[]{:S(2)}) collective-permute-start(f32[2,64,256]{2,1,0:T(8,128)S(1)} %add.164), channel_id=1, source_target_pairs={{0,2},{1,3},{2,0},{3,1},{4,6},{5,7},{6,4},{7,5},{8,10},{9,11},{10,... | collective-permute-start | bytes 393224 | tf_op jit(solution)/shard_map/while/body/eval_jaxpr/ppermute | solution.py:40
  59.5 5.8 %collective-permute-start = (f32[2,64,256]{2,1,0:T(8,128)S(1)}, f32[2,64,256]{2,1,0:T(8,128)S(1)}, u32[]{:S(2)}, u32[]{:S(2)}) collective-permute-start(f32[2,64,256]{2,1,0:T(8,128)S(1)} %convolution_bitcast_fusion.2), channel_id=1, source_target_pairs={{0,1},{1,0},{2,3},{3,2},{4,5},{5,4},{6,7},{7,6},{8,9},{9,8},{10,11... | collective-permute-start | bytes 393224 | tf_op jit(solution)/shard_map/while/body/eval_jaxpr/ppermute | solution.py:40
  65.4 8.7 %collective-permute-start.1 = (f32[2,64,256]{2,1,0:T(8,128)S(1)}, f32[2,64,256]{2,1,0:T(8,128)S(1)}, u32[]{:S(2)}, u32[]{:S(2)}) collective-permute-start(f32[2,64,256]{2,1,0:T(8,128)S(1)} %add.164), channel_id=1, source_target_pairs={{0,2},{1,3},{2,0},{3,1},{4,6},{5,7},{6,4},{7,5},{8,10},{9,11},{10,... | collective-permute-start | bytes 393224 | tf_op jit(solution)/shard_map/while/body/eval_jaxpr/ppermute | solution.py:40
  86.0 5.8 %collective-permute-start = (f32[2,64,256]{2,1,0:T(8,128)S(1)}, f32[2,64,256]{2,1,0:T(8,128)S(1)}, u32[]{:S(2)}, u32[]{:S(2)}) collective-permute-start(f32[2,64,256]{2,1,0:T(8,128)S(1)} %convolution_bitcast_fusion.2), channel_id=1, source_target_pairs={{0,1},{1,0},{2,3},{3,2},{4,5},{5,4},{6,7},{7,6},{8,9},{9,8},{10,11... | collective-permute-start | bytes 393224 | tf_op jit(solution)/shard_map/while/body/eval_jaxpr/ppermute | solution.py:40
  91.9 8.7 %collective-permute-start.1 = (f32[2,64,256]{2,1,0:T(8,128)S(1)}, f32[2,64,256]{2,1,0:T(8,128)S(1)}, u32[]{:S(2)}, u32[]{:S(2)}) collective-permute-start(f32[2,64,256]{2,1,0:T(8,128)S(1)} %add.164), channel_id=1, source_target_pairs={{0,2},{1,3},{2,0},{3,1},{4,6},{5,7},{6,4},{7,5},{8,10},{9,11},{10,... | collective-permute-start | bytes 393224 | tf_op jit(solution)/shard_map/while/body/eval_jaxpr/ppermute | solution.py:40
  113.5 5.8 %collective-permute-start = (f32[2,64,256]{2,1,0:T(8,128)S(1)}, f32[2,64,256]{2,1,0:T(8,128)S(1)}, u32[]{:S(2)}, u32[]{:S(2)}) collective-permute-start(f32[2,64,256]{2,1,0:T(8,128)S(1)} %convolution_bitcast_fusion.2), channel_id=1, source_target_pairs={{0,1},{1,0},{2,3},{3,2},{4,5},{5,4},{6,7},{7,6},{8,9},{9,8},{10,11... | collective-permute-start | bytes 393224 | tf_op jit(solution)/shard_map/while/body/eval_jaxpr/ppermute | solution.py:40
  119.3 8.7 %collective-permute-start.1 = (f32[2,64,256]{2,1,0:T(8,128)S(1)}, f32[2,64,256]{2,1,0:T(8,128)S(1)}, u32[]{:S(2)}, u32[]{:S(2)}) collective-permute-start(f32[2,64,256]{2,1,0:T(8,128)S(1)} %add.164), channel_id=1, source_target_pairs={{0,2},{1,3},{2,0},{3,1},{4,6},{5,7},{6,4},{7,5},{8,10},{9,11},{10,... | collective-permute-start | bytes 393224 | tf_op jit(solution)/shard_map/while/body/eval_jaxpr/ppermute | solution.py:40
  139.9 5.8 %collective-permute-start = (f32[2,64,256]{2,1,0:T(8,128)S(1)}, f32[2,64,256]{2,1,0:T(8,128)S(1)}, u32[]{:S(2)}, u32[]{:S(2)}) collective-permute-start(f32[2,64,256]{2,1,0:T(8,128)S(1)} %convolution_bitcast_fusion.2), channel_id=1, source_target_pairs={{0,1},{1,0},{2,3},{3,2},{4,5},{5,4},{6,7},{7,6},{8,9},{9,8},{10,11... | collective-permute-start | bytes 393224 | tf_op jit(solution)/shard_map/while/body/eval_jaxpr/ppermute | solution.py:40
  145.8 8.7 %collective-permute-start.1 = (f32[2,64,256]{2,1,0:T(8,128)S(1)}, f32[2,64,256]{2,1,0:T(8,128)S(1)}, u32[]{:S(2)}, u32[]{:S(2)}) collective-permute-start(f32[2,64,256]{2,1,0:T(8,128)S(1)} %add.164), channel_id=1, source_target_pairs={{0,2},{1,3},{2,0},{3,1},{4,6},{5,7},{6,4},{7,5},{8,10},{9,11},{10,... | collective-permute-start | bytes 393224 | tf_op jit(solution)/shard_map/while/body/eval_jaxpr/ppermute | solution.py:40
  167.4 5.8 %collective-permute-start = (f32[2,64,256]{2,1,0:T(8,128)S(1)}, f32[2,64,256]{2,1,0:T(8,128)S(1)}, u32[]{:S(2)}, u32[]{:S(2)}) collective-permute-start(f32[2,64,256]{2,1,0:T(8,128)S(1)} %convolution_bitcast_fusion.2), channel_id=1, source_target_pairs={{0,1},{1,0},{2,3},{3,2},{4,5},{5,4},{6,7},{7,6},{8,9},{9,8},{10,11... | collective-permute-start | bytes 393224 | tf_op jit(solution)/shard_map/while/body/eval_jaxpr/ppermute | solution.py:40
  173.2 8.7 %collective-permute-start.1 = (f32[2,64,256]{2,1,0:T(8,128)S(1)}, f32[2,64,256]{2,1,0:T(8,128)S(1)}, u32[]{:S(2)}, u32[]{:S(2)}) collective-permute-start(f32[2,64,256]{2,1,0:T(8,128)S(1)} %add.164), channel_id=1, source_target_pairs={{0,2},{1,3},{2,0},{3,1},{4,6},{5,7},{6,4},{7,5},{8,10},{9,11},{10,... | collective-permute-start | bytes 393224 | tf_op jit(solution)/shard_map/while/body/eval_jaxpr/ppermute | solution.py:40
  193.9 5.8 %collective-permute-start = (f32[2,64,256]{2,1,0:T(8,128)S(1)}, f32[2,64,256]{2,1,0:T(8,128)S(1)}, u32[]{:S(2)}, u32[]{:S(2)}) collective-permute-start(f32[2,64,256]{2,1,0:T(8,128)S(1)} %convolution_bitcast_fusion.2), channel_id=1, source_target_pairs={{0,1},{1,0},{2,3},{3,2},{4,5},{5,4},{6,7},{7,6},{8,9},{9,8},{10,11... | collective-permute-start | bytes 393224 | tf_op jit(solution)/shard_map/while/body/eval_jaxpr/ppermute | solution.py:40
  199.7 8.7 %collective-permute-start.1 = (f32[2,64,256]{2,1,0:T(8,128)S(1)}, f32[2,64,256]{2,1,0:T(8,128)S(1)}, u32[]{:S(2)}, u32[]{:S(2)}) collective-permute-start(f32[2,64,256]{2,1,0:T(8,128)S(1)} %add.164), channel_id=1, source_target_pairs={{0,2},{1,3},{2,0},{3,1},{4,6},{5,7},{6,4},{7,5},{8,10},{9,11},{10,... | collective-permute-start | bytes 393224 | tf_op jit(solution)/shard_map/while/body/eval_jaxpr/ppermute | solution.py:40
  218.9 0.8 copy-start
